TPU v7x, 256 devices: a whole 4x4x8 slice. The times are simulated.
256 devices in a mesh: mode: 64 (over z, y, x_hi), elem: 4 (over x_lo, core).
Axes of the slice: x: 4 (x_hi: 2, x_lo: 2; x = x_hi * 2 + x_lo), y: 4, z: 8, core: 2. Of those that a mesh axis runs over, the one named last changes fastest.
Arguments:
- velocity: float32 [3, 256, 4, 7, 7, 512], P(None, 'mode', None, None, None, 'elem'), may hold values from -0.3 to 0.3
- radial_dx: float32 [4, 7, 7, 512], P(None, None, None, 'elem'), may hold values from 0.5 to 2
- radial_dy: float32 [4, 7, 7, 512], P(None, None, None, 'elem'), may hold values from -0.5 to 0.5
- around_dx: float32 [4, 7, 7, 512], P(None, None, None, 'elem'), may hold values from -0.5 to 0.5
- around_dy: float32 [4, 7, 7, 512], P(None, None, None, 'elem'), may hold values from 0.5 to 2
- jacobian: float32 [4, 7, 7, 512], P(None, None, None, 'elem'), may hold values from 0.5 to 2
Outputs:
- advection: float32 [3, 256, 4, 7, 7, 512], P(None, 'mode', None, None, None, 'elem')
- pressure: float32 [256, 4, 7, 7, 512], P('mode', None, None, None, 'elem')
All inputs are finite; a program needn't handle non-finite values.
Results may differ from a plain program's by a relative error of at most 0.0003.
Values sent between devices are 32-bit elements; how exact they have to be, the bound alone decides.
A program may use at most 192 MiB of HBM per device.

v0:
```python
import functools
import itertools
import math

import jax
import jax.numpy as jnp
import numpy as np
from jax import lax
from jax.experimental import pallas as pl
from jax.experimental.pallas import tpu as pltpu
from jax.sharding import PartitionSpec as P

MESH = pl.DeviceIdType.MESH
NODES = 7
SQUARE = NODES * NODES
LAYERS = 4
ITERS = 3
COMPONENTS = 3
PLANES = 256
MODES = 64
OWN = PLANES // MODES
ELEMS = 4
LANES = 128
CELLS = COMPONENTS * SQUARE * LAYERS
CHUNKS = -(-CELLS // LANES)
PADDED = CHUNKS * LANES
ROWS = CHUNKS * 8
GROUPS = PADDED // 4

spanwise_wave = 2.0 * math.pi / 64.0
time_step = 0.1

VMEM = pltpu.VMEM
DMA = pltpu.SemaphoreType.DMA


def lobatto_rule(count):
    degree = count - 1
    points = np.cos(np.pi * np.arange(count) / degree)
    legendre = np.zeros((count, count))
    for sweep in range(60):
        legendre[:, 0] = 1.0
        legendre[:, 1] = points
        for order in range(2, count):
            legendre[:, order] = (
                (2 * order - 1) * points * legendre[:, order - 1]
                - (order - 1) * legendre[:, order - 2]
            ) / order
        points = points - (points * legendre[:, degree] - legendre[:, degree - 1]) / (
            count * legendre[:, degree]
        )
    legendre[:, 0] = 1.0
    legendre[:, 1] = points
    for order in range(2, count):
        legendre[:, order] = (
            (2 * order - 1) * points * legendre[:, order - 1] - (order - 1) * legendre[:, order - 2]
        ) / order
    weights = 2.0 / (degree * count * legendre[:, degree] ** 2)
    return (points[::-1].copy(), weights[::-1].copy())


def derivative_table():
    lobatto_nodes = lobatto_rule(NODES)[0]
    total = lobatto_nodes.shape[0]
    scales = np.ones(total)
    for column in range(total):
        for other in range(total):
            if other != column:
                scales[column] = scales[column] / (lobatto_nodes[column] - lobatto_nodes[other])
    table = np.zeros((total, total))
    for row in range(total):
        for column in range(total):
            if row != column:
                table[row, column] = (
                    scales[column] / scales[row] / (lobatto_nodes[row] - lobatto_nodes[column])
                )
        table[row, row] = -np.sum(table[row])
    return table


TABLE = derivative_table().astype(np.float32)
WEIGHTS = lobatto_rule(NODES)[1]


def split(value):
    high = value.astype(jnp.bfloat16)
    return (high, (value - high.astype(jnp.float32)).astype(jnp.bfloat16))


def constant_split(value):
    value = value.astype(np.float32)
    high = value.astype(jnp.bfloat16)
    return (high, (value - high.astype(np.float32)).astype(jnp.bfloat16))


def transform_tables():
    position = np.arange(PLANES)
    plane = np.arange(PLANES)
    order = plane // 2
    angle = 2.0 * np.pi / PLANES * ((position[:, None] * order[None, :]) % PLANES)
    is_sine = (plane % 2 == 1)[None, :]
    is_top = (plane == 1)[None, :]
    parity = np.cos(np.pi * (position % 2))[:, None]
    basis = np.where(is_top, parity, np.where(is_sine, np.sin(angle), np.cos(angle)))
    scaling = np.where(order == 0, 1.0, 2.0) / PLANES
    inverse = (basis * scaling[None, :]).T
    wave = (order * spanwise_wave)[None, :]
    slope = np.where(is_sine, wave * np.cos(angle), -wave * np.sin(angle))
    forward = np.concatenate([basis.T, slope.T], axis=1)
    turned = inverse.reshape(MODES, OWN, PLANES).transpose(1, 0, 2).reshape(PLANES, PLANES)
    return (*constant_split(forward), *constant_split(turned))


def swap_halves(value):
    return pltpu.roll(value, 4, value.ndim - 2)


def halves(first, second):
    lower = lax.broadcasted_iota(jnp.int32, first.shape, first.ndim - 2) < 4
    return (
        jnp.where(lower, first, swap_halves(second)),
        jnp.where(lower, swap_halves(first), second),
    )


def pack_kernel(velocity, out, rows):
    for p in range(OWN):
        for c in range(COMPONENTS):
            start = (c * OWN + p) * SQUARE * LAYERS
            rows[p, pl.ds(c * SQUARE * LAYERS, SQUARE * LAYERS), :] = velocity[
                pl.ds(start, SQUARE * LAYERS), :
            ]
        rows[p, pl.ds(CELLS, PADDED - CELLS), :] = jnp.zeros((PADDED - CELLS, LANES), jnp.float32)
        for k in range(CHUNKS):
            turned = rows[p, pl.ds(k * LANES, LANES), :].T
            for t in range(2):
                out[pl.ds(k * 8 + t * 4 + p, MODES, stride=ROWS), :] = turned[
                    t * MODES : (t + 1) * MODES
                ]


def pack(velocity):
    return pl.pallas_call(
        pack_kernel,
        out_shape=jax.ShapeDtypeStruct((MODES * ROWS, LANES), jnp.float32),
        in_specs=[pl.BlockSpec(memory_space=VMEM)],
        out_specs=pl.BlockSpec(memory_space=VMEM),
        scratch_shapes=[VMEM((OWN, PADDED, LANES), jnp.float32)],
        name="pack",
    )(velocity)


def shifted(me, offset):
    z, y, x = (me // 8, lax.rem(me // 2, 4), lax.rem(me, 2))
    dz, dy, dx = offset
    return lax.rem(z + dz, 8) * 8 + lax.rem(y + dy, 4) * 2 + lax.rem(x + dx, 2)


def exchange_order():
    return [o for o in itertools.product(range(8), range(4), range(2)) if o != (0, 0, 0)]


def exchange_kernel(source, target, own_sem, send_sem, receive_sem):
    me = lax.axis_index("mode")
    barrier = pltpu.get_barrier_semaphore()
    order = exchange_order()
    for offset in order:
        pl.semaphore_signal(
            barrier, inc=1, device_id={"mode": shifted(me, offset)}, device_id_type=MESH
        )
    pl.semaphore_wait(barrier, len(order))
    copies = []
    for index, offset in enumerate(order):
        other = shifted(me, offset)
        copy = pltpu.make_async_remote_copy(
            src_ref=source.at[other],
            dst_ref=target.at[me],
            send_sem=send_sem.at[index],
            recv_sem=receive_sem.at[index],
            device_id={"mode": other},
            device_id_type=MESH,
        )
        copy.start()
        copies.append(copy)
    own = pltpu.make_async_copy(source.at[me], target.at[me], own_sem)
    own.start()
    for copy in copies:
        copy.wait()
    own.wait()


def exchange(value, identity):
    return pl.pallas_call(
        exchange_kernel,
        out_shape=jax.ShapeDtypeStruct((MODES, ROWS, LANES), jnp.float32),
        in_specs=[pl.BlockSpec(memory_space=VMEM)],
        out_specs=pl.BlockSpec(memory_space=VMEM),
        scratch_shapes=[DMA, DMA((MODES,)), DMA((MODES,))],
        compiler_params=pltpu.CompilerParams(collective_id=identity, has_side_effects=True),
        name="exchange%d" % identity,
    )(value)


def three_pass(first, second, dims):
    (a, b), (c, d) = (first, second)
    dot = functools.partial(
        lax.dot_general,
        dimension_numbers=(dims, ((), ())),
        preferred_element_type=jnp.float32,
    )
    return dot(a, c) + (dot(a, d) + dot(b, c))


def advect_kernel(received, metrics, forward_high, forward_low, back_high, back_low, out,
                  planes, values, local, result):
    me = lax.axis_index("mode")
    for k in range(CHUNKS):
        block = received[:, pl.ds(k * 8, 8), :].reshape(MODES // 2, 2, 8, LANES)
        pair = halves(block[:, 0], block[:, 1])
        for t in range(2):
            planes[t, :, pl.ds(k * LANES, LANES)] = pair[t].reshape(PLANES, LANES)
    forward = (forward_high[...], forward_low[...])
    sides = []
    for t in range(2):
        sides.append(three_pass(split(planes[t]), forward, ((0,), (0,))))
    first, second = halves(
        sides[0].reshape(PADDED // 8, 8, 2 * PLANES), sides[1].reshape(PADDED // 8, 8, 2 * PLANES)
    )
    for q in range(PADDED // 8):
        values[2 * q] = first[q]
        values[2 * q + 1] = second[q]
    lane = lax.broadcasted_iota(jnp.int32, (SQUARE, 8, LANES), 2)
    sub = lax.broadcasted_iota(jnp.int32, (SQUARE, 8, LANES), 1)
    chosen = lane == me + jnp.where(sub < 4, 0, MODES)
    for i in range(4):
        picked = jnp.sum(jnp.where(chosen, metrics[i], 0.0), axis=2, keepdims=True)
        local[i] = jnp.broadcast_to(-picked, (SQUARE, 8, LANES))
    zero = jnp.zeros((8, PLANES), jnp.float32)
    for a in range(NODES):
        for b in range(NODES):
            node = a * NODES + b
            mx, my, nx, ny = (jnp.concatenate([local[i, node]] * 2, axis=1) for i in range(4))
            u = values[node, :, :PLANES]
            v = values[SQUARE + node, :, :PLANES]
            w = values[2 * SQUARE + node, :, :PLANES]
            along = u * mx + v * my
            across = u * nx + v * ny
            for c in range(COMPONENTS):
                radial, beside = (zero, zero)
                for i in range(NODES):
                    radial += float(TABLE[a, i]) * values[c * SQUARE + i * NODES + b, :, :PLANES]
                    beside += float(TABLE[b, i]) * values[c * SQUARE + a * NODES + i, :, :PLANES]
                slope = values[c * SQUARE + node, :, PLANES:]
                result[c * SQUARE + node] = radial * along + beside * across - slope * w
    for g in range(COMPONENTS * SQUARE, GROUPS):
        result[g] = zero
    paired = result[...].reshape(GROUPS // 2, 2, 8, PLANES)
    sides = halves(paired[:, 0], paired[:, 1])
    back = (back_high[...], back_low[...])
    for t in range(2):
        spectral = three_pass(back, split(sides[t].reshape(PADDED, PLANES)), ((1,), (1,)))
        for p in range(OWN):
            for k in range(CHUNKS):
                out[pl.ds(k * 8 + t * 4 + p, MODES, stride=ROWS), :] = spectral[
                    p * MODES : (p + 1) * MODES, k * LANES : (k + 1) * LANES
                ]


def advect(received, metrics):
    tables = transform_tables()
    return pl.pallas_call(
        advect_kernel,
        out_shape=jax.ShapeDtypeStruct((MODES * ROWS, LANES), jnp.float32),
        in_specs=[pl.BlockSpec(memory_space=VMEM)] * 6,
        out_specs=pl.BlockSpec(memory_space=VMEM),
        scratch_shapes=[
            VMEM((2, PLANES, PADDED), jnp.float32),
            VMEM((GROUPS, 8, 2 * PLANES), jnp.float32),
            VMEM((4, SQUARE, 8, LANES), jnp.float32),
            VMEM((GROUPS, 8, PLANES), jnp.float32),
        ],
        compiler_params=pltpu.CompilerParams(vmem_limit_bytes=40 << 20),
        name="advect",
    )(received, metrics, *(jnp.asarray(t) for t in tables))


def unpack_kernel(returned, velocity, advection, predicted, rows):
    for p in range(OWN):
        for k in range(CHUNKS):
            block = jnp.concatenate(
                [returned[pl.ds(k * 8 + t * 4 + p, MODES, stride=ROWS), :] for t in range(2)],
                axis=0,
            )
            rows[p, pl.ds(k * LANES, LANES), :] = block.T
        for c in range(COMPONENTS):
            start = (c * OWN + p) * SQUARE * LAYERS
            own = pl.ds(c * SQUARE * LAYERS, SQUARE * LAYERS)
            there = rows[p, own, :]
            advection[pl.ds(start, SQUARE * LAYERS), :] = there
            rows[p, own, :] = velocity[pl.ds(start, SQUARE * LAYERS), :] + time_step * there
    for pair in range(OWN // 2):
        first, second = halves(
            rows[2 * pair].reshape(PADDED // 8, 8, LANES),
            rows[2 * pair + 1].reshape(PADDED // 8, 8, LANES),
        )
        for q in range(PADDED // 8):
            predicted[pair, 2 * q] = first[q]
            predicted[pair, 2 * q + 1] = second[q]


def unpack(returned, velocity):
    return pl.pallas_call(
        unpack_kernel,
        out_shape=(
            jax.ShapeDtypeStruct(velocity.shape, jnp.float32),
            jax.ShapeDtypeStruct((OWN // 2, GROUPS, 8, LANES), jnp.float32),
        ),
        in_specs=[pl.BlockSpec(memory_space=VMEM)] * 2,
        out_specs=(pl.BlockSpec(memory_space=VMEM),) * 2,
        scratch_shapes=[VMEM((OWN, PADDED, LANES), jnp.float32)],
        name="unpack",
    )(returned, velocity)


def contract(matrix, field, axis):
    size = NODES
    if axis == 0:
        return [
            functools.reduce(
                lambda x, y: x + y, [float(matrix[i, j]) * field[j] for j in range(size)]
            )
            for i in range(size)
        ]
    return [
        jnp.stack(
            [
                functools.reduce(
                    lambda x, y: x + y, [float(matrix[i, j]) * slab[j] for j in range(size)]
                )
                for i in range(size)
            ]
        )
        for slab in field
    ]


def pressure_kernel(predicted, metrics, out, stiff, rhs, residual, direction, along, local,
                    radial_s, around_s, rims, posts, send_sem, receive_sem):
    me = lax.axis_index("mode")
    here = lax.axis_index("elem")
    barrier = pltpu.get_barrier_semaphore()
    for step in range(1, ELEMS):
        pl.semaphore_signal(
            barrier, inc=1, device_id={"elem": lax.rem(here + step, ELEMS)}, device_id_type=MESH
        )
    pl.semaphore_wait(barrier, ELEMS - 1)

    sub = lax.broadcasted_iota(jnp.int32, (8, LANES), 0)
    lane = lax.broadcasted_iota(jnp.int32, (8, LANES), 1)
    layer = lax.rem(sub, 4)
    even = sub < 4
    inside = layer < LAYERS - 1
    above = layer > 0
    pairs = range(OWN // 2)
    nodes = range(NODES)

    for a in nodes:
        for b in nodes:
            node = a * NODES + b
            rx, ry, ax, ay, jac = (metrics[i, node] for i in range(5))
            mass = float(np.float32(WEIGHTS[a] * WEIGHTS[b])) * jac
            stiff[0, a, b] = mass * (rx * rx + ry * ry)
            stiff[1, a, b] = mass * (rx * ax + ry * ay)
            stiff[2, a, b] = mass * (ax * ax + ay * ay)
            stiff[3, a, b] = mass

    orders = [(me * (OWN // 2) + pair).astype(jnp.float32) for pair in pairs]
    waves = [jnp.full((8, LANES), order) * spanwise_wave for order in orders]
    tops = [
        jnp.where((jnp.full((8, LANES), order) == 0.0) & (sub >= 4), float(PLANES // 2), order)
        * spanwise_wave
        for order in orders
    ]
    shifts = [top * top for top in tops]

    def radial_of(read, a):
        return functools.reduce(
            lambda x, y: x + y, [float(TABLE[a, i]) * read(i) for i in nodes]
        )

    def around_of(slab):
        return [
            functools.reduce(lambda x, y: x + y, [float(TABLE[b, i]) * slab[i] for i in nodes])
            for b in nodes
        ]

    for pair in pairs:
        wave = jnp.where(even, waves[pair], -waves[pair])
        for a in nodes:
            def component(c, i):
                return predicted[pair, pl.ds(c * SQUARE + i * NODES, NODES)]
            radial = [radial_of(functools.partial(component, c), a) for c in range(2)]
            beside = [around_of(component(c, a)) for c in range(2)]
            third = component(2, a)
            for b in nodes:
                node = a * NODES + b
                rx, ry, ax, ay = (metrics[i, node] for i in range(4))
                divergence = (
                    (rx * radial[0][b] + ax * beside[0][b])
                    + (ry * radial[1][b] + ay * beside[1][b])
                    + wave * swap_halves(third[b])
                )
                local[pair, a, b] = -(stiff[3, a, b] * divergence) / time_step

    def across_layers():
        for pair in pairs:
            low, high = (local[pair, 0], local[pair, NODES - 1])
            other = [pltpu.roll(high[b], 1, 0) for b in nodes]
            this = [pltpu.roll(low[b], 7, 0) for b in nodes]
            for b in nodes:
                local[pair, 0, b] = low[b] + jnp.where(above, other[b], 0.0)
                local[pair, NODES - 1, b] = jnp.where(inside, high[b] + this[b], 0.0)

    def talk(phase, dots):
        first = jnp.zeros((8, LANES), jnp.float32)
        last = jnp.zeros((8, LANES), jnp.float32)
        if phase < ITERS:
            for pair in pairs:
                for a in nodes:
                    slot = pair * NODES + a
                    start = local[pair, a, 0]
                    end = local[pair, a, NODES - 1]
                    first = jnp.where(lane == slot, pltpu.roll(start, slot, 1) if slot else start, first)
                    last = jnp.where(lane == slot, pltpu.roll(end, slot + 1, 1), last)
        for index, dot in enumerate(dots):
            total = jnp.sum(dot, axis=1, keepdims=True)
            first = jnp.where(lane == 2 * 8 + index, total, first)
        posts[phase, 0] = first
        posts[phase, 1] = last
        rims[phase, here, 0] = first
        rims[phase, here, 1] = last
        copies = []
        for step in range(1, ELEMS):
            copy = pltpu.make_async_remote_copy(
                src_ref=posts.at[phase],
                dst_ref=rims.at[phase, here],
                send_sem=send_sem.at[phase, step],
                recv_sem=receive_sem.at[phase, step],
                device_id={"elem": lax.rem(here + step, ELEMS)},
                device_id_type=MESH,
            )
            copy.start()
            copies.append(copy)
        for copy in copies:
            copy.wait()
        total = (rims[phase, 0, 0] + rims[phase, 1, 0]) + (rims[phase, 2, 0] + rims[phase, 3, 0])
        sums = []
        for index in range(len(dots)):
            column = jnp.sum(jnp.where(lane == 2 * 8 + index, total, 0.0), axis=1, keepdims=True)
            column = jnp.broadcast_to(column, (8, LANES))
            lower = jnp.sum(jnp.where(even, column, 0.0), axis=0, keepdims=True)
            upper = jnp.sum(jnp.where(even, 0.0, column), axis=0, keepdims=True)
            sums.append(jnp.where(even, lower, upper))
        right = rims[phase, lax.rem(here + 1, ELEMS), 0]
        left = rims[phase, lax.rem(here + ELEMS - 1, ELEMS), 1]
        return (sums, left, right)

    def across_columns(pair, a, left, right):
        slot = pair * NODES + a
        start = local[pair, a, 0]
        end = local[pair, a, NODES - 1]
        after = jnp.where(
            lane == LANES - 1, pltpu.roll(right, LANES - 1 - slot, 1), pltpu.roll(start, LANES - 1, 1)
        )
        before = jnp.where(
            lane == 0, pltpu.roll(left, (LANES - slot) % LANES, 1) if slot else left, pltpu.roll(end, 1, 1)
        )
        return (start + before, end + after)

    across_layers()
    _, left, right = talk(0, [])
    for pair in pairs:
        for a in nodes:
            start, end = across_columns(pair, a, left, right)
            for b in nodes:
                value = start if b == 0 else end if b == NODES - 1 else local[pair, a, b]
                residual[pair, a, b] = value

    weight_a = [
        jnp.where(above, 0.5, 1.0) if a == 0 else jnp.where(inside, 0.5, 0.0) if a == NODES - 1 else None
        for a in nodes
    ]

    gamma_old = [None, None]
    inner_old = [None, None]
    for turn in range(ITERS):
        dots = []
        for pair in pairs:
            norm = jnp.zeros((8, LANES), jnp.float32)
            for a in nodes:
                slab = residual[pair, a]
                radial = radial_of(lambda i: residual[pair, i], a)
                beside = around_of(slab)
                row = jnp.zeros((8, LANES), jnp.float32)
                for b in nodes:
                    g11, g12, g22 = (stiff[i, a, b] for i in range(3))
                    radial_s[a, b] = g11 * radial[b] + g12 * beside[b]
                    around_s[a, b] = g12 * radial[b] + g22 * beside[b]
                    square = slab[b] * slab[b]
                    row = row + (0.5 * square if b in (0, NODES - 1) else square)
                norm = norm + (row if weight_a[a] is None else row * weight_a[a])
            product = jnp.zeros((8, LANES), jnp.float32)
            for a in nodes:
                spread = functools.reduce(
                    lambda x, y: x + y, [float(TABLE[i, a]) * radial_s[i] for i in nodes]
                )
                slab = around_s[a]
                for b in nodes:
                    beside = functools.reduce(
                        lambda x, y: x + y, [float(TABLE[j, b]) * slab[j] for j in nodes]
                    )
                    here_now = residual[pair, a, b]
                    value = spread[b] + beside + shifts[pair] * stiff[3, a, b] * here_now
                    local[pair, a, b] = value
                    product = product + here_now * value
            dots += [norm, product]
        if turn < ITERS - 1:
            across_layers()
        sums, left, right = talk(turn + 1, dots)
        for pair in pairs:
            gamma, delta = (sums[2 * pair], sums[2 * pair + 1])
            if turn == 0:
                beta, inner = (None, delta)
            else:
                beta = gamma / gamma_old[pair]
                inner = delta - beta * beta * inner_old[pair]
            alpha = gamma / inner
            gamma_old[pair], inner_old[pair] = (gamma, inner)
            for a in nodes:
                if turn < ITERS - 1:
                    start, end = across_columns(pair, a, left, right)
                for b in nodes:
                    now = residual[pair, a, b]
                    if turn:
                        now = now + beta * direction[pair, a, b]
                    step = alpha * now
                    out[pair, a, b] = step if turn == 0 else out[pair, a, b] + step
                    if turn < ITERS - 1:
                        direction[pair, a, b] = now
                        image = start if b == 0 else end if b == NODES - 1 else local[pair, a, b]
                        if turn:
                            image = image + beta * along[pair, a, b]
                        along[pair, a, b] = image
                        residual[pair, a, b] = residual[pair, a, b] - alpha * image


def pressure_of(predicted, metrics):
    field = VMEM((OWN // 2, NODES, NODES, 8, LANES), jnp.float32)
    slabs = VMEM((NODES, NODES, 8, LANES), jnp.float32)
    return pl.pallas_call(
        pressure_kernel,
        out_shape=jax.ShapeDtypeStruct((OWN // 2, NODES, NODES, 8, LANES), jnp.float32),
        in_specs=[pl.BlockSpec(memory_space=VMEM)] * 2,
        out_specs=pl.BlockSpec(memory_space=VMEM),
        scratch_shapes=[
            VMEM((4, NODES, NODES, 8, LANES), jnp.float32),
            VMEM((8, LANES), jnp.float32),
            field,
            field,
            field,
            field,
            slabs,
            slabs,
            VMEM((ITERS + 1, ELEMS, 2, 8, LANES), jnp.float32),
            VMEM((ITERS + 1, 2, 8, LANES), jnp.float32),
            DMA((ITERS + 1, ELEMS)),
            DMA((ITERS + 1, ELEMS)),
        ],
        compiler_params=pltpu.CompilerParams(collective_id=3, has_side_effects=True),
        name="pressure",
    )(predicted, metrics)


def on_device(velocity, radial_dx, radial_dy, around_dx, around_dy, jacobian):
    rows = velocity.transpose(0, 1, 3, 4, 2, 5).reshape(COMPONENTS * OWN * SQUARE * LAYERS, LANES)
    metrics = jnp.stack(
        [
            item.transpose(1, 2, 0, 3).reshape(SQUARE, LAYERS, LANES)
            for item in (radial_dx, radial_dy, around_dx, around_dy, jacobian)
        ]
    )
    metrics = jnp.concatenate([metrics, metrics], axis=2)
    packed = pack(rows).reshape(MODES, ROWS, LANES)
    received = exchange(packed, 1)
    answer = advect(received, metrics).reshape(MODES, ROWS, LANES)
    returned = exchange(answer, 2).reshape(MODES * ROWS, LANES)
    advection, predicted = unpack(returned, rows)
    pressure = pressure_of(predicted, metrics)
    advection = advection.reshape(COMPONENTS, OWN, NODES, NODES, LAYERS, LANES)
    advection = advection.transpose(0, 1, 4, 2, 3, 5)
    pressure = pressure.reshape(OWN // 2, NODES, NODES, 2, LAYERS, LANES)
    pressure = pressure.transpose(0, 3, 4, 1, 2, 5).reshape(OWN, LAYERS, NODES, NODES, LANES)
    return (advection, pressure)


def solution(mesh):
    metric = P(None, None, None, "elem")
    return jax.shard_map(
        on_device,
        mesh=mesh,
        in_specs=(P(None, "mode", None, None, None, "elem"),) + (metric,) * 5,
        out_specs=(P(None, "mode", None, None, None, "elem"), P("mode", None, None, None, "elem")),
        check_vma=False,
    )
```

profile of v0, /device:TPU:1, one launch (start us, length us, event | category | flops | bytes accessed | tf_op | source)
XLA Modules:
  0.0 127.0 jit_solution(1645060236777347326)
XLA Ops:
  0.6 0.9 constant_dynamic-update-slice_fusion.4
  1.5 0.9 constant_dynamic-update-slice_fusion.3
  2.4 0.9 constant_dynamic-update-slice_fusion.2
  3.4 0.9 constant_dynamic-update-slice_fusion.1
  4.3 0.9 constant_dynamic-update-slice_fusion
  5.2 0.2 pad_maximum_fusion.metrics
  5.4 0.0 copy-start
  5.4 3.2 %pack.1 = f32[2560,128]{1,0:T(8,128)} custom-call(f32[2352,128]{1,0:T(8,128)} %bitcast.31), custom_call_target="tpu_custom_call" | custom-call | tf_op jit(solution)/shard_map/pack/pallas_call | solution.py:143
  8.5 0.0 copy-start.3
  8.5 0.0 copy-start.4
  8.5 0.0 copy-start.5
  8.5 0.0 copy-start.6
  8.5 46.2 %exchange1.1.received = f32[64,40,128]{2,1,0:T(8,128)} custom-call(f32[64,40,128]{2,1,0:T(8,128)} %bitcast.30), custom_call_target="tpu_custom_call" | custom-call | tf_op jit(solution)/shard_map/exchange1/pallas_call | solution.py:193
  54.8 0.0 copy-done
  54.8 0.0 copy-done.3
  54.8 0.0 copy-done.4
  54.8 0.0 copy-done.5
  54.8 0.0 copy-done.6
  54.8 0.0 copy-start.1
  54.9 1.3 %copy-done.1 = f32[64,40,128]{2,1,0:T(8,128)S(1)} copy-done((f32[64,40,128]{2,1,0:T(8,128)S(1)}, f32[64,40,128]{2,1,0:T(8,128)}, u32[]{:S(2)}) %copy-start.1) | copy-done | bytes 1310744
  56.2 3.8 %advect.1 = f32[2560,128]{1,0:T(8,128)S(1)} custom-call(f32[64,40,128]{2,1,0:T(8,128)S(1)} %copy-done.1, f32[5,49,8,128]{3,2,1,0:T(8,128)S(1)} %pad_maximum_fusion.metrics, bf16[256,512]{1,0:T(8,128)(2,1)S(1)} %copy-done.4, bf16[256,512]{1,0:T(8,128)(2,1)S(1)} %copy-done.3, bf16[256,256]{1,0:T(8,128)(2,1)S(1)} %copy-done.6, bf16[256,256]{1,0:T(8,128)(2,1)S(1)} %copy-done.5), custom_call_target="tpu_custom_call" | custom-call | tf_op jit(solution)/shard_map/advect/pallas_call | solution.py:271
  59.9 0.0 copy-start.2
  60.0 1.1 copy-done.2
  61.0 39.2 %exchange2.1 = f32[64,40,128]{2,1,0:T(8,128)} custom-call(f32[64,40,128]{2,1,0:T(8,128)} %bitcast.28), custom_call_target="tpu_custom_call" | custom-call | tf_op jit(solution)/shard_map/exchange2/pallas_call | solution.py:193
  100.2 3.7 %unpack.1 = (f32[2352,128]{1,0:T(8,128)}, f32[2,160,8,128]{3,2,1,0:T(8,128)}) custom-call(f32[2560,128]{1,0:T(8,128)} %bitcast.29, f32[2352,128]{1,0:T(8,128)} %bitcast.32), custom_call_target="tpu_custom_call" | custom-call | tf_op jit(solution)/shard_map/unpack/pallas_call | solution.py:312
  103.9 21.3 %pressure.1 = f32[2,7,7,8,128]{4,3,2,1,0:T(8,128)} custom-call(f32[2,160,8,128]{3,2,1,0:T(8,128)} %get-tuple-element.5.predicted, f32[5,49,8,128]{3,2,1,0:T(8,128)} %copy-done), custom_call_target="tpu_custom_call" | custom-call | tf_op jit(solution)/shard_map/pressure/pallas_call | solution.py:560
  125.2 1.8 %copy.12 = f32[2,2,4,7,7,128]{5,2,4,3,1,0:T(4,128)} copy(f32[2,2,4,7,7,128]{5,2,1,4,3,0:T(4,128)} %bitcast.33) | data formatting | bytes 802816 | tf_op jit(solution)/shard_map/transpose | solution.py:602
Async XLA Ops:
  5.4 49.4 %copy-start = (f32[5,49,8,128]{3,2,1,0:T(8,128)}, f32[5,49,8,128]{3,2,1,0:T(8,128)S(1)}, u32[]{:S(2)}) copy-start(f32[5,49,8,128]{3,2,1,0:T(8,128)S(1)} %pad_maximum_fusion.metrics) | copy-start | bytes 3010564
  8.5 46.3 %copy-start.3 = (bf16[256,512]{1,0:T(8,128)(2,1)S(1)}, bf16[256,512]{1,0:T(8,128)(2,1)}, u32[]{:S(2)}) copy-start(bf16[256,512]{1,0:T(8,128)(2,1)} %constant.9.clone.forward_low) | copy-start | bytes 786436
  8.5 46.3 %copy-start.4 = (bf16[256,512]{1,0:T(8,128)(2,1)S(1)}, bf16[256,512]{1,0:T(8,128)(2,1)}, u32[]{:S(2)}) copy-start(bf16[256,512]{1,0:T(8,128)(2,1)} %constant.8.clone.forward_high) | copy-start | bytes 786436
  8.5 46.3 %copy-start.5 = (bf16[256,256]{1,0:T(8,128)(2,1)S(1)}, bf16[256,256]{1,0:T(8,128)(2,1)}, u32[]{:S(2)}) copy-start(bf16[256,256]{1,0:T(8,128)(2,1)} %constant.11.clone.back_low) | copy-start | bytes 393220
  8.5 46.3 %copy-start.6 = (bf16[256,256]{1,0:T(8,128)(2,1)S(1)}, bf16[256,256]{1,0:T(8,128)(2,1)}, u32[]{:S(2)}) copy-start(bf16[256,256]{1,0:T(8,128)(2,1)} %constant.10.clone.back_high) | copy-start | bytes 393220
  54.8 1.3 %copy-start.1 = (f32[64,40,128]{2,1,0:T(8,128)S(1)}, f32[64,40,128]{2,1,0:T(8,128)}, u32[]{:S(2)}) copy-start(f32[64,40,128]{2,1,0:T(8,128)} %exchange1.1.received) | copy-start | bytes 3932164
  59.9 1.1 copy-start.2
where the time goes:
time: 127 us
  Pallas kernels  117 us (92%)
  local copies, waits for them, and re-layouts  8.75 us (7%)
    pallas_call x2, Pallas kernels, exchange(): pl.pallas_call(exchange_kernel, out_shape=jax.ShapeDtypeStruct((MODES, RO...  85.4 us
    pallas_call x1, Pallas kernels, pressure_of(): pl.pallas_call(pressure_kernel, out_shape=jax.ShapeDtypeStruct((OWN // 2,...  21.3 us
    unnamed x18, local copies, waits for them, and re-layouts  6.02 us
    pallas_call x1, Pallas kernels, advect(): pl.pallas_call(advect_kernel, out_shape=jax.ShapeDtypeStruct((MODES * ROW...  3.78 us
    pallas_call x1, Pallas kernels, unpack(): pl.pallas_call(unpack_kernel, out_shape=(jax.ShapeDtypeStruct(velocity.sh...  3.67 us
    pallas_call x1, Pallas kernels, pack(): pl.pallas_call(pack_kernel, out_shape=jax.ShapeDtypeStruct((MODES * ROWS,...  3.16 us

commit v1 on v0

v1 whole, which is shorter than its diff:
```python
import functools
import itertools
import math

import jax
import jax.numpy as jnp
import numpy as np
from jax import lax
from jax.experimental import pallas as pl
from jax.experimental.pallas import tpu as pltpu
from jax.sharding import PartitionSpec as P

MESH = pl.DeviceIdType.MESH
NODES = 7
SQUARE = NODES * NODES
LAYERS = 4
ITERS = 3
COMPONENTS = 3
PLANES = 256
MODES = 64
OWN = PLANES // MODES
ELEMS = 4
LANES = 128
CELLS = COMPONENTS * SQUARE * LAYERS
CHUNKS = -(-CELLS // LANES)
PADDED = CHUNKS * LANES
HALF = MODES * CHUNKS * OWN
GROUPS = PADDED // 4

spanwise_wave = 2.0 * math.pi / 64.0
time_step = 0.1

VMEM = pltpu.VMEM
DMA = pltpu.SemaphoreType.DMA


def lobatto_rule(count):
    degree = count - 1
    points = np.cos(np.pi * np.arange(count) / degree)
    legendre = np.zeros((count, count))
    for sweep in range(60):
        legendre[:, 0] = 1.0
        legendre[:, 1] = points
        for order in range(2, count):
            legendre[:, order] = (
                (2 * order - 1) * points * legendre[:, order - 1]
                - (order - 1) * legendre[:, order - 2]
            ) / order
        points = points - (points * legendre[:, degree] - legendre[:, degree - 1]) / (
            count * legendre[:, degree]
        )
    legendre[:, 0] = 1.0
    legendre[:, 1] = points
    for order in range(2, count):
        legendre[:, order] = (
            (2 * order - 1) * points * legendre[:, order - 1] - (order - 1) * legendre[:, order - 2]
        ) / order
    weights = 2.0 / (degree * count * legendre[:, degree] ** 2)
    return (points[::-1].copy(), weights[::-1].copy())


def derivative_table():
    lobatto_nodes = lobatto_rule(NODES)[0]
    total = lobatto_nodes.shape[0]
    scales = np.ones(total)
    for column in range(total):
        for other in range(total):
            if other != column:
                scales[column] = scales[column] / (lobatto_nodes[column] - lobatto_nodes[other])
    table = np.zeros((total, total))
    for row in range(total):
        for column in range(total):
            if row != column:
                table[row, column] = (
                    scales[column] / scales[row] / (lobatto_nodes[row] - lobatto_nodes[column])
                )
        table[row, row] = -np.sum(table[row])
    return table


TABLE = derivative_table().astype(np.float32)
WEIGHTS = lobatto_rule(NODES)[1]


def split(value):
    high = value.astype(jnp.bfloat16)
    return (high, (value - high.astype(jnp.float32)).astype(jnp.bfloat16))


def constant_split(value):
    value = value.astype(np.float32)
    high = value.astype(jnp.bfloat16)
    return (high, (value - high.astype(np.float32)).astype(jnp.bfloat16))


def transform_tables():
    position = np.arange(PLANES)
    plane = np.arange(PLANES)
    order = plane // 2
    angle = 2.0 * np.pi / PLANES * ((position[:, None] * order[None, :]) % PLANES)
    is_sine = (plane % 2 == 1)[None, :]
    is_top = (plane == 1)[None, :]
    parity = np.cos(np.pi * (position % 2))[:, None]
    basis = np.where(is_top, parity, np.where(is_sine, np.sin(angle), np.cos(angle)))
    scaling = np.where(order == 0, 1.0, 2.0) / PLANES
    inverse = (basis * scaling[None, :]).T
    wave = (order * spanwise_wave)[None, :]
    slope = np.where(is_sine, wave * np.cos(angle), -wave * np.sin(angle))
    forward = np.concatenate([basis.T, slope.T], axis=1)
    turned = inverse.reshape(MODES, OWN, PLANES).transpose(1, 0, 2).reshape(PLANES, PLANES)
    return (*constant_split(forward), *constant_split(turned))


def swap_halves(value):
    return pltpu.roll(value, 4, value.ndim - 2)


def halves(first, second):
    lower = lax.broadcasted_iota(jnp.int32, first.shape, first.ndim - 2) < 4
    return (
        jnp.where(lower, first, swap_halves(second)),
        jnp.where(lower, swap_halves(first), second),
    )


def shifted(me, step):
    z, y, x = (me // 8, lax.rem(me // 2, 4), lax.rem(me, 2))
    dz, dy, dx = (step // 8, lax.rem(step // 2, 4), lax.rem(step, 2))
    return lax.rem(z + dz, 8) * 8 + lax.rem(y + dy, 4) * 2 + lax.rem(x + dx, 2)


def three_pass(first, second, dims):
    (a, b), (c, d) = (first, second)
    dot = functools.partial(
        lax.dot_general,
        dimension_numbers=(dims, ((), ())),
        preferred_element_type=jnp.float32,
    )
    return dot(a, c) + (dot(a, d) + dot(b, c))


def send_all(source, target, send_sem, receive_sem, me):
    def one(step, carry):
        other = shifted(me, step)
        pltpu.make_async_remote_copy(
            src_ref=source.at[other],
            dst_ref=target.at[me],
            send_sem=send_sem,
            recv_sem=receive_sem,
            device_id={"mode": other},
            device_id_type=MESH,
        ).start()
        return carry

    lax.fori_loop(1, MODES, one, 0)
    target[me] = source[me]


def wait_all(buffer, sem):
    others = buffer.at[pl.ds(0, MODES - 1)]
    pltpu.make_async_copy(others, others, sem).wait()


def step_kernel(velocity, radial_dx, radial_dy, around_dx, around_dy, jacobian,
                forward_high, forward_low, back_high, back_low, advection, out,
                rows, posted, got, answer, returned, local, values, result, predicted,
                fields, edges, geometry, tables, metrics, stiff, residual, direction, along,
                image_raw, radial_s, around_s, rims, posts,
                load_sem, store_sem, send_sem, receive_sem, rim_send_sem, rim_receive_sem):
    loads = [pltpu.make_async_copy(velocity, fields, load_sem.at[0])]
    for i, metric in enumerate((radial_dx, radial_dy, around_dx, around_dy, jacobian)):
        loads.append(pltpu.make_async_copy(metric, geometry.at[i], load_sem.at[1 + i]))
    for i, table in enumerate((forward_high, forward_low)):
        loads.append(pltpu.make_async_copy(table, tables.at[i], load_sem.at[6 + i]))
    for i, table in enumerate((back_high, back_low)):
        loads.append(pltpu.make_async_copy(table, edges.at[i], load_sem.at[8 + i]))
    for load in loads:
        load.start()
    me = lax.axis_index("mode")
    barrier = pltpu.get_barrier_semaphore()

    def greet(step, carry):
        pl.semaphore_signal(
            barrier, inc=1, device_id={"mode": shifted(me, step)}, device_id_type=MESH
        )
        return carry

    lax.fori_loop(1, MODES, greet, 0)
    here = lax.axis_index("elem")
    for step in range(1, ELEMS):
        pl.semaphore_signal(
            barrier, inc=1, device_id={"elem": lax.rem(here + step, ELEMS)}, device_id_type=MESH
        )
    loads[0].wait()

    outgoing = posted.reshape(2 * MODES * CHUNKS * OWN, LANES)
    for p in range(OWN):
        for c in range(COMPONENTS):
            start = (c * OWN + p) * SQUARE * LAYERS
            rows[p, pl.ds(c * SQUARE * LAYERS, SQUARE * LAYERS), :] = fields[
                pl.ds(start, SQUARE * LAYERS), :
            ]
        rows[p, pl.ds(CELLS, PADDED - CELLS), :] = jnp.zeros((PADDED - CELLS, LANES), jnp.float32)
        for k in range(CHUNKS):
            turned = rows[p, pl.ds(k * LANES, LANES), :].T
            for t in range(2):
                outgoing[pl.ds(t * HALF + k * OWN + p, MODES, stride=CHUNKS * OWN), :] = turned[
                    t * MODES : (t + 1) * MODES
                ]
    pl.semaphore_wait(barrier, MODES - 1 + ELEMS - 1)
    for t in range(2):
        send_all(posted.at[t], got.at[t], send_sem.at[0, t], receive_sem.at[0, t], me)

    for load in loads[1:]:
        load.wait()
    lane = lax.broadcasted_iota(jnp.int32, (SQUARE, LAYERS, LANES), 2)
    for t in range(2):
        for i in range(4):
            chosen = jnp.where(lane == me + t * MODES, geometry[i], 0.0)
            picked = jnp.sum(chosen, axis=2, keepdims=True)
            local[t, i] = jnp.broadcast_to(-picked, (SQUARE, LAYERS, LANES))

    sub = lax.broadcasted_iota(jnp.int32, (8, LANES), 0)
    lane = lax.broadcasted_iota(jnp.int32, (8, LANES), 1)
    layer = lax.rem(sub, 4)
    even = sub < 4
    inside = layer < LAYERS - 1
    above = layer > 0
    pairs = range(OWN // 2)
    nodes = range(NODES)

    for i in range(5):
        metrics[i] = jnp.concatenate([geometry[i]] * 2, axis=1)

    for a in nodes:
        for b in nodes:
            node = a * NODES + b
            rx, ry, ax, ay, jac = (metrics[i, node] for i in range(5))
            mass = float(np.float32(WEIGHTS[a] * WEIGHTS[b])) * jac
            stiff[0, a, b] = mass * (rx * rx + ry * ry)
            stiff[1, a, b] = mass * (rx * ax + ry * ay)
            stiff[2, a, b] = mass * (ax * ax + ay * ay)
            stiff[3, a, b] = mass

    zero = jnp.zeros((LAYERS, PLANES), jnp.float32)
    for g in range(COMPONENTS * SQUARE, GROUPS):
        result[g] = zero
    answers = answer.reshape(2 * MODES * CHUNKS * OWN, LANES)

    def advect(t, carry):
        wait_all(got.at[t], receive_sem.at[0, t])
        planes = jnp.concatenate(
            [got[t, :, k].reshape(PLANES, LANES) for k in range(CHUNKS)], axis=1
        )
        physical = three_pass(split(planes), (tables[0], tables[1]), ((0,), (0,)))
        values[...] = physical.reshape(GROUPS, LAYERS, 2 * PLANES)
        for a in range(NODES):
            for b in range(NODES):
                node = a * NODES + b
                mx, my, nx, ny = (
                    jnp.concatenate([local[t, i, node]] * 2, axis=1) for i in range(4)
                )
                u = values[node, :, :PLANES]
                v = values[SQUARE + node, :, :PLANES]
                w = values[2 * SQUARE + node, :, :PLANES]
                along = u * mx + v * my
                across = u * nx + v * ny
                for c in range(COMPONENTS):
                    radial, beside = (zero, zero)
                    for i in range(NODES):
                        radial += float(TABLE[a, i]) * values[c * SQUARE + i * NODES + b, :, :PLANES]
                        beside += float(TABLE[b, i]) * values[c * SQUARE + a * NODES + i, :, :PLANES]
                    slope = values[c * SQUARE + node, :, PLANES:]
                    result[c * SQUARE + node] = radial * along + beside * across - slope * w
        spectral = three_pass(
            (edges[0], edges[1]),
            split(result[...].reshape(PADDED, PLANES)),
            ((1,), (1,)),
        )
        for p in range(OWN):
            for k in range(CHUNKS):
                answers[pl.ds(t * HALF + k * OWN + p, MODES, stride=CHUNKS * OWN), :] = spectral[
                    p * MODES : (p + 1) * MODES, k * LANES : (k + 1) * LANES
                ]
        send_all(answer.at[t], returned.at[t], send_sem.at[1, t], receive_sem.at[1, t], me)
        return carry

    lax.fori_loop(0, 2, advect, 0)
    for t in range(2):
        wait_all(returned.at[t], receive_sem.at[1, t])

    incoming = returned.reshape(2 * MODES * CHUNKS * OWN, LANES)
    for p in range(OWN):
        for k in range(CHUNKS):
            block = jnp.concatenate(
                [
                    incoming[pl.ds(t * HALF + k * OWN + p, MODES, stride=CHUNKS * OWN), :]
                    for t in range(2)
                ],
                axis=0,
            )
            rows[p, pl.ds(k * LANES, LANES), :] = block.T
        for c in range(COMPONENTS):
            there = pl.ds((c * OWN + p) * SQUARE * LAYERS, SQUARE * LAYERS)
            own = pl.ds(c * SQUARE * LAYERS, SQUARE * LAYERS)
            term = rows[p, own, :]
            rows[p, own, :] = fields[there, :] + time_step * term
            fields[there, :] = term
    store = pltpu.make_async_copy(fields, advection, store_sem)
    store.start()
    for pair in range(OWN // 2):
        first, second = halves(
            rows[2 * pair].reshape(PADDED // 8, 8, LANES),
            rows[2 * pair + 1].reshape(PADDED // 8, 8, LANES),
        )
        for q in range(PADDED // 8):
            predicted[pair, 2 * q] = first[q]
            predicted[pair, 2 * q + 1] = second[q]

    orders = [(me * (OWN // 2) + pair).astype(jnp.float32) for pair in pairs]
    waves = [jnp.full((8, LANES), order) * spanwise_wave for order in orders]
    tops = [
        jnp.where((jnp.full((8, LANES), order) == 0.0) & (sub >= 4), float(PLANES // 2), order)
        * spanwise_wave
        for order in orders
    ]
    shifts = [top * top for top in tops]

    def radial_of(read, a):
        return functools.reduce(
            lambda x, y: x + y, [float(TABLE[a, i]) * read(i) for i in nodes]
        )

    def around_of(slab):
        return [
            functools.reduce(lambda x, y: x + y, [float(TABLE[b, i]) * slab[i] for i in nodes])
            for b in nodes
        ]

    for pair in pairs:
        wave = jnp.where(even, waves[pair], -waves[pair])
        for a in nodes:
            def component(c, i):
                return predicted[pair, pl.ds(c * SQUARE + i * NODES, NODES)]
            radial = [radial_of(functools.partial(component, c), a) for c in range(2)]
            beside = [around_of(component(c, a)) for c in range(2)]
            third = component(2, a)
            for b in nodes:
                node = a * NODES + b
                rx, ry, ax, ay = (metrics[i, node] for i in range(4))
                divergence = (
                    (rx * radial[0][b] + ax * beside[0][b])
                    + (ry * radial[1][b] + ay * beside[1][b])
                    + wave * swap_halves(third[b])
                )
                image_raw[pair, a, b] = -(stiff[3, a, b] * divergence) / time_step

    def across_layers():
        for pair in pairs:
            low, high = (image_raw[pair, 0], image_raw[pair, NODES - 1])
            other = [pltpu.roll(high[b], 1, 0) for b in nodes]
            this = [pltpu.roll(low[b], 7, 0) for b in nodes]
            for b in nodes:
                image_raw[pair, 0, b] = low[b] + jnp.where(above, other[b], 0.0)
                image_raw[pair, NODES - 1, b] = jnp.where(inside, high[b] + this[b], 0.0)

    def talk(phase, dots):
        first = jnp.zeros((8, LANES), jnp.float32)
        last = jnp.zeros((8, LANES), jnp.float32)
        if phase < ITERS:
            for pair in pairs:
                for a in nodes:
                    slot = pair * NODES + a
                    start = image_raw[pair, a, 0]
                    end = image_raw[pair, a, NODES - 1]
                    first = jnp.where(lane == slot, pltpu.roll(start, slot, 1) if slot else start, first)
                    last = jnp.where(lane == slot, pltpu.roll(end, slot + 1, 1), last)
        for index, dot in enumerate(dots):
            total = jnp.sum(dot, axis=1, keepdims=True)
            first = jnp.where(lane == 2 * 8 + index, total, first)
        posts[phase, 0] = first
        posts[phase, 1] = last
        rims[phase, here, 0] = first
        rims[phase, here, 1] = last
        copies = []
        for step in range(1, ELEMS):
            copy = pltpu.make_async_remote_copy(
                src_ref=posts.at[phase],
                dst_ref=rims.at[phase, here],
                send_sem=rim_send_sem.at[phase, step],
                recv_sem=rim_receive_sem.at[phase, step],
                device_id={"elem": lax.rem(here + step, ELEMS)},
                device_id_type=MESH,
            )
            copy.start()
            copies.append(copy)
        for copy in copies:
            copy.wait()
        total = (rims[phase, 0, 0] + rims[phase, 1, 0]) + (rims[phase, 2, 0] + rims[phase, 3, 0])
        sums = []
        for index in range(len(dots)):
            column = jnp.sum(jnp.where(lane == 2 * 8 + index, total, 0.0), axis=1, keepdims=True)
            column = jnp.broadcast_to(column, (8, LANES))
            lower = jnp.sum(jnp.where(even, column, 0.0), axis=0, keepdims=True)
            upper = jnp.sum(jnp.where(even, 0.0, column), axis=0, keepdims=True)
            sums.append(jnp.where(even, lower, upper))
        right = rims[phase, lax.rem(here + 1, ELEMS), 0]
        left = rims[phase, lax.rem(here + ELEMS - 1, ELEMS), 1]
        return (sums, left, right)

    def across_columns(pair, a, left, right):
        slot = pair * NODES + a
        start = image_raw[pair, a, 0]
        end = image_raw[pair, a, NODES - 1]
        after = jnp.where(
            lane == LANES - 1, pltpu.roll(right, LANES - 1 - slot, 1), pltpu.roll(start, LANES - 1, 1)
        )
        before = jnp.where(
            lane == 0, pltpu.roll(left, (LANES - slot) % LANES, 1) if slot else left, pltpu.roll(end, 1, 1)
        )
        return (start + before, end + after)

    across_layers()
    _, left, right = talk(0, [])
    for pair in pairs:
        for a in nodes:
            start, end = across_columns(pair, a, left, right)
            for b in nodes:
                value = start if b == 0 else end if b == NODES - 1 else image_raw[pair, a, b]
                residual[pair, a, b] = value

    weight_a = [
        jnp.where(above, 0.5, 1.0) if a == 0 else jnp.where(inside, 0.5, 0.0) if a == NODES - 1 else None
        for a in nodes
    ]

    gamma_old = [None, None]
    inner_old = [None, None]
    for turn in range(ITERS):
        dots = []
        for pair in pairs:
            norm = jnp.zeros((8, LANES), jnp.float32)
            for a in nodes:
                slab = residual[pair, a]
                radial = radial_of(lambda i: residual[pair, i], a)
                beside = around_of(slab)
                row = jnp.zeros((8, LANES), jnp.float32)
                for b in nodes:
                    g11, g12, g22 = (stiff[i, a, b] for i in range(3))
                    radial_s[a, b] = g11 * radial[b] + g12 * beside[b]
                    around_s[a, b] = g12 * radial[b] + g22 * beside[b]
                    square = slab[b] * slab[b]
                    row = row + (0.5 * square if b in (0, NODES - 1) else square)
                norm = norm + (row if weight_a[a] is None else row * weight_a[a])
            product = jnp.zeros((8, LANES), jnp.float32)
            for a in nodes:
                spread = functools.reduce(
                    lambda x, y: x + y, [float(TABLE[i, a]) * radial_s[i] for i in nodes]
                )
                slab = around_s[a]
                for b in nodes:
                    beside = functools.reduce(
                        lambda x, y: x + y, [float(TABLE[j, b]) * slab[j] for j in nodes]
                    )
                    here_now = residual[pair, a, b]
                    value = spread[b] + beside + shifts[pair] * stiff[3, a, b] * here_now
                    image_raw[pair, a, b] = value
                    product = product + here_now * value
            dots += [norm, product]
        if turn < ITERS - 1:
            across_layers()
        sums, left, right = talk(turn + 1, dots)
        for pair in pairs:
            gamma, delta = (sums[2 * pair], sums[2 * pair + 1])
            if turn == 0:
                beta, inner = (None, delta)
            else:
                beta = gamma / gamma_old[pair]
                inner = delta - beta * beta * inner_old[pair]
            alpha = gamma / inner
            gamma_old[pair], inner_old[pair] = (gamma, inner)
            for a in nodes:
                if turn < ITERS - 1:
                    start, end = across_columns(pair, a, left, right)
                for b in nodes:
                    now = residual[pair, a, b]
                    if turn:
                        now = now + beta * direction[pair, a, b]
                    step = alpha * now
                    total = step if turn == 0 else predicted[pair, a * NODES + b] + step
                    if turn == ITERS - 1:
                        for h in range(2):
                            out[2 * pair + h, a * NODES + b] = total[h * LAYERS : (h + 1) * LAYERS]
                    else:
                        predicted[pair, a * NODES + b] = total
                    if turn < ITERS - 1:
                        direction[pair, a, b] = now
                        image = start if b == 0 else end if b == NODES - 1 else image_raw[pair, a, b]
                        if turn:
                            image = image + beta * along[pair, a, b]
                        along[pair, a, b] = image
                        residual[pair, a, b] = residual[pair, a, b] - alpha * image

    store.wait()
    for t in range(2):
        wait_all(posted.at[t], send_sem.at[0, t])
        wait_all(answer.at[t], send_sem.at[1, t])


def step_of(velocity, *metrics):
    tables = transform_tables()
    blocks = VMEM((2, MODES, CHUNKS, OWN, LANES), jnp.float32)
    field = VMEM((OWN // 2, NODES, NODES, 8, LANES), jnp.float32)
    slabs = VMEM((NODES, NODES, 8, LANES), jnp.float32)
    return pl.pallas_call(
        step_kernel,
        out_shape=(
            jax.ShapeDtypeStruct(velocity.shape, jnp.float32),
            jax.ShapeDtypeStruct((OWN, SQUARE, LAYERS, LANES), jnp.float32),
        ),
        in_specs=[pl.BlockSpec(memory_space=pltpu.HBM)] * 10,
        out_specs=(pl.BlockSpec(memory_space=pltpu.HBM), pl.BlockSpec(memory_space=VMEM)),
        scratch_shapes=[
            VMEM((OWN, PADDED, LANES), jnp.float32),
            blocks,
            blocks,
            blocks,
            blocks,
            VMEM((2, 4, SQUARE, LAYERS, LANES), jnp.float32),
            VMEM((GROUPS, LAYERS, 2 * PLANES), jnp.float32),
            VMEM((GROUPS, LAYERS, PLANES), jnp.float32),
            VMEM((OWN // 2, GROUPS, 8, LANES), jnp.float32),
            VMEM(velocity.shape, jnp.float32),
            VMEM((2, PLANES, PLANES), jnp.bfloat16),
            VMEM((5, SQUARE, LAYERS, LANES), jnp.float32),
            VMEM((2, PLANES, 2 * PLANES), jnp.bfloat16),
            VMEM((5, SQUARE, 8, LANES), jnp.float32),
            VMEM((4, NODES, NODES, 8, LANES), jnp.float32),
            field,
            field,
            field,
            field,
            slabs,
            slabs,
            VMEM((ITERS + 1, ELEMS, 2, 8, LANES), jnp.float32),
            VMEM((ITERS + 1, 2, 8, LANES), jnp.float32),
            DMA((10,)),
            DMA,
            DMA((2, 2)),
            DMA((2, 2)),
            DMA((ITERS + 1, ELEMS)),
            DMA((ITERS + 1, ELEMS)),
        ],
        compiler_params=pltpu.CompilerParams(
            collective_id=1, has_side_effects=True, vmem_limit_bytes=60 << 20
        ),
        name="step",
    )(velocity, *metrics, *(jnp.asarray(t) for t in tables))


def on_device(velocity, radial_dx, radial_dy, around_dx, around_dy, jacobian):
    rows = velocity.transpose(0, 1, 3, 4, 2, 5).reshape(COMPONENTS * OWN * SQUARE * LAYERS, LANES)
    metrics = [
        item.transpose(1, 2, 0, 3).reshape(SQUARE, LAYERS, LANES)
        for item in (radial_dx, radial_dy, around_dx, around_dy, jacobian)
    ]
    advection, pressure = step_of(rows, *metrics)
    advection = advection.reshape(COMPONENTS, OWN, NODES, NODES, LAYERS, LANES)
    pressure = pressure.reshape(OWN, NODES, NODES, LAYERS, LANES)
    return (advection.transpose(0, 1, 4, 2, 3, 5), pressure.transpose(0, 3, 1, 2, 4))


def solution(mesh):
    metric = P(None, None, None, "elem")
    return jax.shard_map(
        on_device,
        mesh=mesh,
        in_specs=(P(None, "mode", None, None, None, "elem"),) + (metric,) * 5,
        out_specs=(P(None, "mode", None, None, None, "elem"), P("mode", None, None, None, "elem")),
        check_vma=False,
    )
```

time: 127 us -> 93.7 us (0.74)
  Pallas kernels: 117 us -> 89.8 us
  local copies, waits for them, and re-layouts: 8.75 us -> 3.2 us
    pallas_call x6 -> x1, Pallas kernels: 117 us -> 89.8 us  [step_of(): pl.pallas_call(step_kernel, out_shape=(jax.ShapeDtypeStruct(velocity.shap...]
    unnamed x18 -> x4, local copies, waits for them, and re-layouts: 6.02 us -> 3.2 us
    transpose x1 -> x0, local copies, waits for them, and re-layouts: 1.82 us -> none  [on_device(): pressure.transpose(0, 3, 4, 1, 2, 5)]
where the time goes in v1:
time: 93.7 us; the launch traced here: 93.6 us
  Pallas kernels  89.8 us (96%)
  local copies, waits for them, and re-layouts  3.2 us (3%)
    pallas_call x1, Pallas kernels, step_of(): pl.pallas_call(step_kernel, out_shape=(jax.ShapeDtypeStruct(velocity.shap...  89.8 us
    unnamed x4, local copies, waits for them, and re-layouts  3.2 us

profile of v1, /device:TPU:1, one launch (start us, length us, event | category | flops | bytes accessed | tf_op | source)
XLA Modules:
  0.0 93.6 jit_solution(1217376264739514111)
XLA Ops:
  0.6 89.8 %step.1 = (f32[2352,128]{1,0:T(8,128)}, f32[4,49,4,128]{3,2,1,0:T(4,128)}) custom-call(f32[2352,128]{1,0:T(8,128)} %bitcast.25, f32[49,4,128]{2,1,0:T(4,128)} %bitcast.27, f32[49,4,128]{2,1,0:T(4,128)} %bitcast.28, f32[49,4,128]{2,1,0:T(4,128)} %bitcast.29, f32[49,4,128]{2,1,0:T(4,128)} %bitcast.30, f32[49,4,128]{2,1,0:T(4,128)} %bitcast.31, ...), custom_call_target="tpu_custom_call" | custom-call | tf_op jit(solution)/shard_map/step/pallas_call | solution.py:515
  90.4 0.0 copy-start
  90.4 2.4 %copy.14 = f32[3,4,4,7,7,128]{5,2,4,3,1,0:T(4,128)} copy(f32[3,4,4,7,7,128]{5,2,4,3,1,0:T(4,128)} %bitcast.24) | data formatting | bytes 2408448
  92.9 0.0 copy-done
  92.9 0.7 copy.15
Async XLA Ops:
  90.4 2.5 %copy-start = (f32[4,49,4,128]{3,2,1,0:T(4,128)S(1)}, f32[4,49,4,128]{3,2,1,0:T(4,128)}, u32[]{:S(2)}) copy-start(f32[4,49,4,128]{3,2,1,0:T(4,128)} %get-tuple-element.5) | copy-start | bytes 1204228

commit v2 on v1

--- a/solution.py
+++ b/solution.py
@@ -24,7 +24,12 @@
 CELLS = COMPONENTS * SQUARE * LAYERS
 CHUNKS = -(-CELLS // LANES)
 PADDED = CHUNKS * LANES
-HALF = MODES * CHUNKS * OWN
+FULL = CELLS // LANES
+REST = CELLS - FULL * LANES
+SPARE = LANES - REST
+TAIL = REST - SPARE
+LARGE = FULL * OWN + 3
+SMALL = FULL * OWN + 2
 GROUPS = PADDED // 4
 
 spanwise_wave = 2.0 * math.pi / 64.0
@@ -107,8 +112,28 @@
     wave = (order * spanwise_wave)[None, :]
     slope = np.where(is_sine, wave * np.cos(angle), -wave * np.sin(angle))
     forward = np.concatenate([basis.T, slope.T], axis=1)
+    forward = forward.reshape(MODES, OWN, 2 * PLANES).transpose(1, 0, 2).reshape(PLANES, 2 * PLANES)
     turned = inverse.reshape(MODES, OWN, PLANES).transpose(1, 0, 2).reshape(PLANES, PLANES)
     return (*constant_split(forward), *constant_split(turned))
+
+
+def contract(matrix, field):
+    last, half = (NODES - 1, NODES // 2)
+    even = [field[j] + field[last - j] for j in range(half)]
+    odd = [field[j] - field[last - j] for j in range(half)]
+
+    def total(terms):
+        return functools.reduce(lambda x, y: x + y, terms)
+
+    out = [None] * NODES
+    for i in range(half):
+        minus = [0.5 * (float(matrix[i, j]) - float(matrix[i, last - j])) for j in range(half)]
+        plus = [0.5 * (float(matrix[i, j]) + float(matrix[i, last - j])) for j in range(half)]
+        p = total([minus[j] * odd[j] for j in range(half)])
+        q = total([plus[j] * even[j] for j in range(half)] + [float(matrix[i, half]) * field[half]])
+        out[i], out[last - i] = (p + q, p - q)
+    out[half] = total([float(matrix[half, j]) * odd[j] for j in range(half)])
+    return out
 
 
 def swap_halves(value):
@@ -123,9 +148,11 @@
     )
 
 
-def shifted(me, step):
+def partner(me, step):
     z, y, x = (me // 8, lax.rem(me // 2, 4), lax.rem(me, 2))
-    dz, dy, dx = (step // 8, lax.rem(step // 2, 4), lax.rem(step, 2))
+    turn_z, rest = (step // 8, 7 - lax.rem(step, 8))
+    dz = 4 + turn_z // 2 - lax.rem(turn_z, 2) * (turn_z // 2 + (turn_z + 1) // 2)
+    dy, dx = (rest // 2, lax.rem(rest, 2))
     return lax.rem(z + dz, 8) * 8 + lax.rem(y + dy, 4) * 2 + lax.rem(x + dx, 2)
 
 
@@ -139,9 +166,56 @@
     return dot(a, c) + (dot(a, d) + dot(b, c))
 
 
+def rows_of(ref):
+    return ref.reshape(MODES * ref.shape[1], LANES)
+
+
+def put(ref, row, value):
+    rows_of(ref)[pl.ds(row, MODES, stride=ref.shape[1]), :] = value
+
+
+def take(ref, row):
+    return rows_of(ref)[pl.ds(row, MODES, stride=ref.shape[1]), :]
+
+
+def before(bound, first, second):
+    lane = lax.broadcasted_iota(jnp.int32, first.shape, 1)
+    return jnp.where(lane < bound, first, second)
+
+
+def turn(value, amount):
+    return pltpu.roll(value, amount % LANES, 1)
+
+
+def put_large(ref, x, small_rest):
+    put(ref, FULL * OWN, before(REST, x[0], turn(x[3], REST)))
+    put(ref, FULL * OWN + 1, before(REST, x[1], turn(x[3], TAIL)))
+    rest = before(REST + TAIL, turn(small_rest[0], TAIL), turn(small_rest[1], 2 * TAIL))
+    put(ref, FULL * OWN + 2, before(REST, x[2], rest))
+
+
+def put_small(ref, y):
+    put(ref, FULL * OWN, before(REST, y[0], turn(y[3], REST)))
+    put(ref, FULL * OWN + 1, before(REST, y[1], turn(y[2], REST)))
+
+
+def take_large(ref):
+    x = [take(ref, FULL * OWN + i) for i in range(3)]
+    return x + [before(SPARE, turn(x[0], -REST), turn(x[1], -TAIL))]
+
+
+def take_small(ref, large):
+    y = [take(ref, FULL * OWN + i) for i in range(2)]
+    rest = take(large, FULL * OWN + 2)
+    return y + [
+        before(SPARE, turn(y[1], -REST), turn(rest, -TAIL)),
+        before(SPARE, turn(y[0], -REST), turn(rest, -2 * TAIL)),
+    ]
+
+
 def send_all(source, target, send_sem, receive_sem, me):
     def one(step, carry):
-        other = shifted(me, step)
+        other = partner(me, step)
         pltpu.make_async_remote_copy(
             src_ref=source.at[other],
             dst_ref=target.at[me],
@@ -152,7 +226,7 @@
         ).start()
         return carry
 
-    lax.fori_loop(1, MODES, one, 0)
+    lax.fori_loop(0, MODES - 1, one, 0)
     target[me] = source[me]
 
 
@@ -163,10 +237,10 @@
 
 def step_kernel(velocity, radial_dx, radial_dy, around_dx, around_dy, jacobian,
                 forward_high, forward_low, back_high, back_low, advection, out,
-                rows, posted, got, answer, returned, local, values, result, predicted,
-                fields, edges, geometry, tables, metrics, stiff, residual, direction, along,
+                rows, posted_0, posted_1, got_0, got_1, answer_0, answer_1, returned_0, returned_1, local, values, result, predicted,
+                fields, edges, geometry, tables, metrics, stiff, residual, direction, carried,
                 image_raw, radial_s, around_s, rims, posts,
-                load_sem, store_sem, send_sem, receive_sem, rim_send_sem, rim_receive_sem):
+                load_sem, send_sem, receive_sem, rim_send_sem, rim_receive_sem):
     loads = [pltpu.make_async_copy(velocity, fields, load_sem.at[0])]
     for i, metric in enumerate((radial_dx, radial_dy, around_dx, around_dy, jacobian)):
         loads.append(pltpu.make_async_copy(metric, geometry.at[i], load_sem.at[1 + i]))
@@ -174,26 +248,29 @@
         loads.append(pltpu.make_async_copy(table, tables.at[i], load_sem.at[6 + i]))
     for i, table in enumerate((back_high, back_low)):
         loads.append(pltpu.make_async_copy(table, edges.at[i], load_sem.at[8 + i]))
-    for load in loads:
-        load.start()
+    loads[0].start()
     me = lax.axis_index("mode")
     barrier = pltpu.get_barrier_semaphore()
 
     def greet(step, carry):
         pl.semaphore_signal(
-            barrier, inc=1, device_id={"mode": shifted(me, step)}, device_id_type=MESH
+            barrier, inc=1, device_id={"mode": partner(me, step)}, device_id_type=MESH
         )
         return carry
 
-    lax.fori_loop(1, MODES, greet, 0)
+    lax.fori_loop(0, MODES - 1, greet, 0)
     here = lax.axis_index("elem")
     for step in range(1, ELEMS):
         pl.semaphore_signal(
             barrier, inc=1, device_id={"elem": lax.rem(here + step, ELEMS)}, device_id_type=MESH
         )
     loads[0].wait()
-
-    outgoing = posted.reshape(2 * MODES * CHUNKS * OWN, LANES)
+    for load in loads[1:]:
+        load.start()
+
+    posted, got = ((posted_0, posted_1), (got_0, got_1))
+    answer, returned = ((answer_0, answer_1), (returned_0, returned_1))
+    last = ([], [])
     for p in range(OWN):
         for c in range(COMPONENTS):
             start = (c * OWN + p) * SQUARE * LAYERS
@@ -204,12 +281,16 @@
         for k in range(CHUNKS):
             turned = rows[p, pl.ds(k * LANES, LANES), :].T
             for t in range(2):
-                outgoing[pl.ds(t * HALF + k * OWN + p, MODES, stride=CHUNKS * OWN), :] = turned[
-                    t * MODES : (t + 1) * MODES
-                ]
+                part = turned[t * MODES : (t + 1) * MODES]
+                if k < FULL:
+                    put(posted[t], k * OWN + p, part)
+                else:
+                    last[t].append(part)
+    put_large(posted_0, last[0], last[1][2:])
+    put_small(posted_1, last[1])
     pl.semaphore_wait(barrier, MODES - 1 + ELEMS - 1)
     for t in range(2):
-        send_all(posted.at[t], got.at[t], send_sem.at[0, t], receive_sem.at[0, t], me)
+        send_all(posted[t], got[t], send_sem.at[0, t], receive_sem.at[0, t], me)
 
     for load in loads[1:]:
         load.wait()
@@ -245,12 +326,17 @@
     zero = jnp.zeros((LAYERS, PLANES), jnp.float32)
     for g in range(COMPONENTS * SQUARE, GROUPS):
         result[g] = zero
-    answers = answer.reshape(2 * MODES * CHUNKS * OWN, LANES)
-
-    def advect(t, carry):
-        wait_all(got.at[t], receive_sem.at[0, t])
+    small_rest = []
+    for t in range(2):
+        wait_all(got[t], receive_sem.at[0, t])
+        rest = take_small(got_1, got_0) if t else take_large(got_0)
         planes = jnp.concatenate(
-            [got[t, :, k].reshape(PLANES, LANES) for k in range(CHUNKS)], axis=1
+            [
+                jnp.concatenate([take(got[t], k * OWN + p) for p in range(OWN)], axis=0)
+                for k in range(FULL)
+            ]
+            + [jnp.concatenate(rest, axis=0)],
+            axis=1,
         )
         physical = three_pass(split(planes), (tables[0], tables[1]), ((0,), (0,)))
         values[...] = physical.reshape(GROUPS, LAYERS, 2 * PLANES)
@@ -277,24 +363,27 @@
             split(result[...].reshape(PADDED, PLANES)),
             ((1,), (1,)),
         )
+        last = []
         for p in range(OWN):
-            for k in range(CHUNKS):
-                answers[pl.ds(t * HALF + k * OWN + p, MODES, stride=CHUNKS * OWN), :] = spectral[
-                    p * MODES : (p + 1) * MODES, k * LANES : (k + 1) * LANES
-                ]
-        send_all(answer.at[t], returned.at[t], send_sem.at[1, t], receive_sem.at[1, t], me)
-        return carry
-
-    lax.fori_loop(0, 2, advect, 0)
+            part = spectral[p * MODES : (p + 1) * MODES]
+            for k in range(FULL):
+                put(answer[t], k * OWN + p, part[:, k * LANES : (k + 1) * LANES])
+            last.append(part[:, FULL * LANES :])
+        if t:
+            put_large(answer_1, last, small_rest)
+        else:
+            put_small(answer_0, last)
+            small_rest = last[2:]
+        send_all(answer[t], returned[t], send_sem.at[1, t], receive_sem.at[1, t], me)
     for t in range(2):
-        wait_all(returned.at[t], receive_sem.at[1, t])
-
-    incoming = returned.reshape(2 * MODES * CHUNKS * OWN, LANES)
+        wait_all(returned[t], receive_sem.at[1, t])
+
+    rest = (take_small(returned_0, returned_1), take_large(returned_1))
     for p in range(OWN):
         for k in range(CHUNKS):
             block = jnp.concatenate(
                 [
-                    incoming[pl.ds(t * HALF + k * OWN + p, MODES, stride=CHUNKS * OWN), :]
+                    take(returned[t], k * OWN + p) if k < FULL else rest[t][p]
                     for t in range(2)
                 ],
                 axis=0,
@@ -305,9 +394,7 @@
             own = pl.ds(c * SQUARE * LAYERS, SQUARE * LAYERS)
             term = rows[p, own, :]
             rows[p, own, :] = fields[there, :] + time_step * term
-            fields[there, :] = term
-    store = pltpu.make_async_copy(fields, advection, store_sem)
-    store.start()
+            advection[there, :] = term
     for pair in range(OWN // 2):
         first, second = halves(
             rows[2 * pair].reshape(PADDED // 8, 8, LANES),
@@ -326,34 +413,29 @@
     ]
     shifts = [top * top for top in tops]
 
-    def radial_of(read, a):
-        return functools.reduce(
-            lambda x, y: x + y, [float(TABLE[a, i]) * read(i) for i in nodes]
-        )
-
-    def around_of(slab):
-        return [
-            functools.reduce(lambda x, y: x + y, [float(TABLE[b, i]) * slab[i] for i in nodes])
-            for b in nodes
-        ]
-
     for pair in pairs:
         wave = jnp.where(even, waves[pair], -waves[pair])
+        for b in nodes:
+            for c, kept in enumerate((radial_s, around_s)):
+                radial = contract(
+                    TABLE, [predicted[pair, c * SQUARE + a * NODES + b] for a in nodes]
+                )
+                for a in nodes:
+                    kept[a, b] = radial[a]
         for a in nodes:
-            def component(c, i):
-                return predicted[pair, pl.ds(c * SQUARE + i * NODES, NODES)]
-            radial = [radial_of(functools.partial(component, c), a) for c in range(2)]
-            beside = [around_of(component(c, a)) for c in range(2)]
-            third = component(2, a)
+            beside = [
+                contract(TABLE, [predicted[pair, c * SQUARE + a * NODES + b] for b in nodes])
+                for c in range(2)
+            ]
             for b in nodes:
                 node = a * NODES + b
                 rx, ry, ax, ay = (metrics[i, node] for i in range(4))
                 divergence = (
-                    (rx * radial[0][b] + ax * beside[0][b])
-                    + (ry * radial[1][b] + ay * beside[1][b])
-                    + wave * swap_halves(third[b])
+                    (rx * radial_s[a, b] + ax * beside[0][b])
+                    + (ry * around_s[a, b] + ay * beside[1][b])
+                    + wave * swap_halves(predicted[pair, 2 * SQUARE + node])
                 )
-                image_raw[pair, a, b] = -(stiff[3, a, b] * divergence) / time_step
+                image_raw[pair, a, b] = (stiff[3, a, b] * divergence) * (-1.0 / time_step)
 
     def across_layers():
         for pair in pairs:
@@ -439,33 +521,35 @@
     for turn in range(ITERS):
         dots = []
         for pair in pairs:
+            for b in nodes:
+                radial = contract(TABLE, [residual[pair, a, b] for a in nodes])
+                for a in nodes:
+                    radial_s[a, b] = radial[a]
             norm = jnp.zeros((8, LANES), jnp.float32)
             for a in nodes:
-                slab = residual[pair, a]
-                radial = radial_of(lambda i: residual[pair, i], a)
-                beside = around_of(slab)
-                row = jnp.zeros((8, LANES), jnp.float32)
+                slab = [residual[pair, a, b] for b in nodes]
+                beside = contract(TABLE, slab)
+                spread = []
                 for b in nodes:
                     g11, g12, g22 = (stiff[i, a, b] for i in range(3))
-                    radial_s[a, b] = g11 * radial[b] + g12 * beside[b]
-                    around_s[a, b] = g12 * radial[b] + g22 * beside[b]
-                    square = slab[b] * slab[b]
-                    row = row + (0.5 * square if b in (0, NODES - 1) else square)
+                    radial = radial_s[a, b]
+                    radial_s[a, b] = g11 * radial + g12 * beside[b]
+                    spread.append(g12 * radial + g22 * beside[b])
+                spread = contract(TABLE.T, spread)
+                squares = [item * item for item in slab]
+                row = 0.5 * (squares[0] + squares[NODES - 1])
+                for b in nodes:
+                    image_raw[pair, a, b] = spread[b] + shifts[pair] * stiff[3, a, b] * slab[b]
+                    if 0 < b < NODES - 1:
+                        row = row + squares[b]
                 norm = norm + (row if weight_a[a] is None else row * weight_a[a])
             product = jnp.zeros((8, LANES), jnp.float32)
-            for a in nodes:
-                spread = functools.reduce(
-                    lambda x, y: x + y, [float(TABLE[i, a]) * radial_s[i] for i in nodes]
-                )
-                slab = around_s[a]
-                for b in nodes:
-                    beside = functools.reduce(
-                        lambda x, y: x + y, [float(TABLE[j, b]) * slab[j] for j in nodes]
-                    )
-                    here_now = residual[pair, a, b]
-                    value = spread[b] + beside + shifts[pair] * stiff[3, a, b] * here_now
+            for b in nodes:
+                radial = contract(TABLE.T, [radial_s[a, b] for a in nodes])
+                for a in nodes:
+                    value = image_raw[pair, a, b] + radial[a]
                     image_raw[pair, a, b] = value
-                    product = product + here_now * value
+                    product = product + residual[pair, a, b] * value
             dots += [norm, product]
         if turn < ITERS - 1:
             across_layers()
@@ -497,19 +581,18 @@
                         direction[pair, a, b] = now
                         image = start if b == 0 else end if b == NODES - 1 else image_raw[pair, a, b]
                         if turn:
-                            image = image + beta * along[pair, a, b]
-                        along[pair, a, b] = image
+                            image = image + beta * carried[pair, a, b]
+                        carried[pair, a, b] = image
                         residual[pair, a, b] = residual[pair, a, b] - alpha * image
 
-    store.wait()
     for t in range(2):
-        wait_all(posted.at[t], send_sem.at[0, t])
-        wait_all(answer.at[t], send_sem.at[1, t])
+        wait_all(posted[t], send_sem.at[0, t])
+        wait_all(answer[t], send_sem.at[1, t])
 
 
 def step_of(velocity, *metrics):
     tables = transform_tables()
-    blocks = VMEM((2, MODES, CHUNKS, OWN, LANES), jnp.float32)
+    large, small = (VMEM((MODES, rows, 1, LANES), jnp.float32) for rows in (LARGE, SMALL))
     field = VMEM((OWN // 2, NODES, NODES, 8, LANES), jnp.float32)
     slabs = VMEM((NODES, NODES, 8, LANES), jnp.float32)
     return pl.pallas_call(
@@ -519,13 +602,17 @@
             jax.ShapeDtypeStruct((OWN, SQUARE, LAYERS, LANES), jnp.float32),
         ),
         in_specs=[pl.BlockSpec(memory_space=pltpu.HBM)] * 10,
-        out_specs=(pl.BlockSpec(memory_space=pltpu.HBM), pl.BlockSpec(memory_space=VMEM)),
+        out_specs=(pl.BlockSpec(memory_space=VMEM),) * 2,
         scratch_shapes=[
             VMEM((OWN, PADDED, LANES), jnp.float32),
-            blocks,
-            blocks,
-            blocks,
-            blocks,
+            large,
+            small,
+            large,
+            small,
+            small,
+            large,
+            small,
+            large,
             VMEM((2, 4, SQUARE, LAYERS, LANES), jnp.float32),
             VMEM((GROUPS, LAYERS, 2 * PLANES), jnp.float32),
             VMEM((GROUPS, LAYERS, PLANES), jnp.float32),
@@ -545,17 +632,21 @@
             VMEM((ITERS + 1, ELEMS, 2, 8, LANES), jnp.float32),
             VMEM((ITERS + 1, 2, 8, LANES), jnp.float32),
             DMA((10,)),
-            DMA,
             DMA((2, 2)),
             DMA((2, 2)),
             DMA((ITERS + 1, ELEMS)),
             DMA((ITERS + 1, ELEMS)),
         ],
         compiler_params=pltpu.CompilerParams(
-            collective_id=1, has_side_effects=True, vmem_limit_bytes=60 << 20
+            collective_id=1, has_side_effects=True, vmem_limit_bytes=40 << 20
         ),
         name="step",
-    )(velocity, *metrics, *(jnp.asarray(t) for t in tables))
+    )(
+        *(
+            pltpu.with_memory_space_constraint(item, pltpu.HBM)
+            for item in (velocity, *metrics, *(jnp.asarray(t) for t in tables))
+        )
+    )
 
 
 def on_device(velocity, radial_dx, radial_dy, around_dx, around_dy, jacobian):

time: 93.7 us -> 85.7 us (0.915)
  Pallas kernels: 89.8 us -> 83.2 us
  local copies, waits for them, and re-layouts: 3.2 us -> 1.77 us
    pallas_call x1, Pallas kernels: 89.8 us -> 83.2 us  [step_of(): pl.pallas_call(step_kernel, out_shape=(jax.ShapeDtypeStruct(velocity.shap...]
    unnamed x4 -> x2, local copies, waits for them, and re-layouts: 3.2 us -> 1.77 us
where the time goes in v2:
time: 85.7 us; the launch traced here: 85.6 us
  Pallas kernels  83.2 us (97%)
  local copies, waits for them, and re-layouts  1.77 us (2%)
    pallas_call x1, Pallas kernels, step_of(): pl.pallas_call(step_kernel, out_shape=(jax.ShapeDtypeStruct(velocity.shap...  83.2 us
    unnamed x2, local copies, waits for them, and re-layouts  1.77 us

profile of v2, /device:TPU:1, one launch (start us, length us, event | category | flops | bytes accessed | tf_op | source)
XLA Modules:
  0.0 85.6 jit_solution(17339453994994504229)
XLA Ops:
  0.6 83.2 %step.1 = (f32[2352,128]{1,0:T(8,128)S(1)}, f32[4,49,4,128]{3,2,1,0:T(4,128)S(1)}) custom-call(f32[2352,128]{1,0:T(8,128)} %bitcast.26, f32[49,4,128]{2,1,0:T(4,128)} %bitcast.27, f32[49,4,128]{2,1,0:T(4,128)} %bitcast.28, f32[49,4,128]{2,1,0:T(4,128)} %bitcast.29, f32[49,4,128]{2,1,0:T(4,128)} %bitcast.30, f32[49,4,128]{2,1,0:T(4,128)} %bitcast.31, ...), custom_call_target="tpu_custom_call" | custom-call | tf_op jit(solution)/shard_map/step/pallas_call | solution.py:598
  83.9 1.0 %copy.14 = f32[3,4,4,7,7,128]{5,2,4,3,1,0:T(4,128)} copy(f32[3,4,4,7,7,128]{5,2,4,3,1,0:T(4,128)S(1)} %bitcast.24) | data formatting | bytes 2408448
  84.9 0.7 copy.15

commit v3 on v2

--- a/solution.py
+++ b/solution.py
@@ -413,7 +413,7 @@
     ]
     shifts = [top * top for top in tops]
 
-    for pair in pairs:
+    def right_side(pair):
         wave = jnp.where(even, waves[pair], -waves[pair])
         for b in nodes:
             for c, kept in enumerate((radial_s, around_s)):
@@ -437,79 +437,66 @@
                 )
                 image_raw[pair, a, b] = (stiff[3, a, b] * divergence) * (-1.0 / time_step)
 
-    def across_layers():
-        for pair in pairs:
-            low, high = (image_raw[pair, 0], image_raw[pair, NODES - 1])
-            other = [pltpu.roll(high[b], 1, 0) for b in nodes]
-            this = [pltpu.roll(low[b], 7, 0) for b in nodes]
-            for b in nodes:
-                image_raw[pair, 0, b] = low[b] + jnp.where(above, other[b], 0.0)
-                image_raw[pair, NODES - 1, b] = jnp.where(inside, high[b] + this[b], 0.0)
-
-    def talk(phase, dots):
+    def across_layers(pair):
+        low = [image_raw[pair, 0, b] for b in nodes]
+        high = [image_raw[pair, NODES - 1, b] for b in nodes]
+        for b in nodes:
+            other, this = (pltpu.roll(high[b], 1, 0), pltpu.roll(low[b], 7, 0))
+            image_raw[pair, 0, b] = low[b] + jnp.where(above, other, 0.0)
+            image_raw[pair, NODES - 1, b] = jnp.where(inside, high[b] + this, 0.0)
+
+    def post(phase, pair, dots):
         first = jnp.zeros((8, LANES), jnp.float32)
-        last = jnp.zeros((8, LANES), jnp.float32)
         if phase < ITERS:
-            for pair in pairs:
-                for a in nodes:
-                    slot = pair * NODES + a
-                    start = image_raw[pair, a, 0]
-                    end = image_raw[pair, a, NODES - 1]
-                    first = jnp.where(lane == slot, pltpu.roll(start, slot, 1) if slot else start, first)
-                    last = jnp.where(lane == slot, pltpu.roll(end, slot + 1, 1), last)
+            for a in nodes:
+                start = image_raw[pair, a, 0]
+                end = image_raw[pair, a, NODES - 1]
+                first = jnp.where(lane == a, pltpu.roll(start, a, 1) if a else start, first)
+                first = jnp.where(lane == 32 + a, pltpu.roll(end, 33 + a, 1), first)
         for index, dot in enumerate(dots):
             total = jnp.sum(dot, axis=1, keepdims=True)
-            first = jnp.where(lane == 2 * 8 + index, total, first)
-        posts[phase, 0] = first
-        posts[phase, 1] = last
-        rims[phase, here, 0] = first
-        rims[phase, here, 1] = last
+            first = jnp.where(lane == 8 + index, total, first)
+        posts[phase, pair] = first
+        rims[phase, pair, here] = first
         copies = []
         for step in range(1, ELEMS):
             copy = pltpu.make_async_remote_copy(
-                src_ref=posts.at[phase],
-                dst_ref=rims.at[phase, here],
-                send_sem=rim_send_sem.at[phase, step],
-                recv_sem=rim_receive_sem.at[phase, step],
+                src_ref=posts.at[phase, pair],
+                dst_ref=rims.at[phase, pair, here],
+                send_sem=rim_send_sem.at[phase, pair, step],
+                recv_sem=rim_receive_sem.at[phase, pair, step],
                 device_id={"elem": lax.rem(here + step, ELEMS)},
                 device_id_type=MESH,
             )
             copy.start()
             copies.append(copy)
+        return copies
+
+    def collect(phase, pair, copies, count):
         for copy in copies:
             copy.wait()
-        total = (rims[phase, 0, 0] + rims[phase, 1, 0]) + (rims[phase, 2, 0] + rims[phase, 3, 0])
+        came = [rims[phase, pair, i] for i in range(ELEMS)]
+        total = (came[0] + came[1]) + (came[2] + came[3])
         sums = []
-        for index in range(len(dots)):
-            column = jnp.sum(jnp.where(lane == 2 * 8 + index, total, 0.0), axis=1, keepdims=True)
+        for index in range(count):
+            column = jnp.sum(jnp.where(lane == 8 + index, total, 0.0), axis=1, keepdims=True)
             column = jnp.broadcast_to(column, (8, LANES))
             lower = jnp.sum(jnp.where(even, column, 0.0), axis=0, keepdims=True)
             upper = jnp.sum(jnp.where(even, 0.0, column), axis=0, keepdims=True)
             sums.append(jnp.where(even, lower, upper))
-        right = rims[phase, lax.rem(here + 1, ELEMS), 0]
-        left = rims[phase, lax.rem(here + ELEMS - 1, ELEMS), 1]
+        right = rims[phase, pair, lax.rem(here + 1, ELEMS)]
+        left = rims[phase, pair, lax.rem(here + ELEMS - 1, ELEMS)]
         return (sums, left, right)
 
     def across_columns(pair, a, left, right):
-        slot = pair * NODES + a
+        slot = a
         start = image_raw[pair, a, 0]
         end = image_raw[pair, a, NODES - 1]
         after = jnp.where(
             lane == LANES - 1, pltpu.roll(right, LANES - 1 - slot, 1), pltpu.roll(start, LANES - 1, 1)
         )
-        before = jnp.where(
-            lane == 0, pltpu.roll(left, (LANES - slot) % LANES, 1) if slot else left, pltpu.roll(end, 1, 1)
-        )
+        before = jnp.where(lane == 0, pltpu.roll(left, LANES - 32 - slot, 1), pltpu.roll(end, 1, 1))
         return (start + before, end + after)
-
-    across_layers()
-    _, left, right = talk(0, [])
-    for pair in pairs:
-        for a in nodes:
-            start, end = across_columns(pair, a, left, right)
-            for b in nodes:
-                value = start if b == 0 else end if b == NODES - 1 else image_raw[pair, a, b]
-                residual[pair, a, b] = value
 
     weight_a = [
         jnp.where(above, 0.5, 1.0) if a == 0 else jnp.where(inside, 0.5, 0.0) if a == NODES - 1 else None
@@ -518,72 +505,90 @@
 
     gamma_old = [None, None]
     inner_old = [None, None]
-    for turn in range(ITERS):
-        dots = []
+    def apply(pair):
+        for b in nodes:
+            radial = contract(TABLE, [residual[pair, a, b] for a in nodes])
+            for a in nodes:
+                radial_s[a, b] = radial[a]
+        norm = jnp.zeros((8, LANES), jnp.float32)
+        for a in nodes:
+            slab = [residual[pair, a, b] for b in nodes]
+            beside = contract(TABLE, slab)
+            spread = []
+            for b in nodes:
+                g11, g12, g22 = (stiff[i, a, b] for i in range(3))
+                radial = radial_s[a, b]
+                radial_s[a, b] = g11 * radial + g12 * beside[b]
+                spread.append(g12 * radial + g22 * beside[b])
+            spread = contract(TABLE.T, spread)
+            squares = [item * item for item in slab]
+            row = 0.5 * (squares[0] + squares[NODES - 1])
+            for b in nodes:
+                image_raw[pair, a, b] = spread[b] + shifts[pair] * stiff[3, a, b] * slab[b]
+                if 0 < b < NODES - 1:
+                    row = row + squares[b]
+            norm = norm + (row if weight_a[a] is None else row * weight_a[a])
+        product = jnp.zeros((8, LANES), jnp.float32)
+        for b in nodes:
+            radial = contract(TABLE.T, [radial_s[a, b] for a in nodes])
+            for a in nodes:
+                value = image_raw[pair, a, b] + radial[a]
+                image_raw[pair, a, b] = value
+                product = product + residual[pair, a, b] * value
+        return [norm, product]
+
+    def update(turn, pair, sums, left, right):
+        gamma, delta = sums
+        if turn == 0:
+            beta, inner = (None, delta)
+        else:
+            beta = gamma / gamma_old[pair]
+            inner = delta - beta * beta * inner_old[pair]
+        alpha = gamma / inner
+        gamma_old[pair], inner_old[pair] = (gamma, inner)
+        for a in nodes:
+            if turn < ITERS - 1:
+                start, end = across_columns(pair, a, left, right)
+            for b in nodes:
+                now = residual[pair, a, b]
+                if turn:
+                    now = now + beta * direction[pair, a, b]
+                step = alpha * now
+                total = step if turn == 0 else predicted[pair, a * NODES + b] + step
+                if turn == ITERS - 1:
+                    for h in range(2):
+                        out[2 * pair + h, a * NODES + b] = total[h * LAYERS : (h + 1) * LAYERS]
+                else:
+                    predicted[pair, a * NODES + b] = total
+                if turn < ITERS - 1:
+                    direction[pair, a, b] = now
+                    image = start if b == 0 else end if b == NODES - 1 else image_raw[pair, a, b]
+                    if turn:
+                        image = image + beta * carried[pair, a, b]
+                    carried[pair, a, b] = image
+                    residual[pair, a, b] = residual[pair, a, b] - alpha * image
+
+    copies = [None, None]
+    for pair in pairs:
+        right_side(pair)
+        across_layers(pair)
+        copies[pair] = post(0, pair, [])
+    for phase in range(ITERS + 1):
         for pair in pairs:
-            for b in nodes:
-                radial = contract(TABLE, [residual[pair, a, b] for a in nodes])
+            sums, left, right = collect(phase, pair, copies[pair], 2 if phase else 0)
+            if phase:
+                update(phase - 1, pair, sums, left, right)
+            else:
                 for a in nodes:
-                    radial_s[a, b] = radial[a]
-            norm = jnp.zeros((8, LANES), jnp.float32)
-            for a in nodes:
-                slab = [residual[pair, a, b] for b in nodes]
-                beside = contract(TABLE, slab)
-                spread = []
-                for b in nodes:
-                    g11, g12, g22 = (stiff[i, a, b] for i in range(3))
-                    radial = radial_s[a, b]
-                    radial_s[a, b] = g11 * radial + g12 * beside[b]
-                    spread.append(g12 * radial + g22 * beside[b])
-                spread = contract(TABLE.T, spread)
-                squares = [item * item for item in slab]
-                row = 0.5 * (squares[0] + squares[NODES - 1])
-                for b in nodes:
-                    image_raw[pair, a, b] = spread[b] + shifts[pair] * stiff[3, a, b] * slab[b]
-                    if 0 < b < NODES - 1:
-                        row = row + squares[b]
-                norm = norm + (row if weight_a[a] is None else row * weight_a[a])
-            product = jnp.zeros((8, LANES), jnp.float32)
-            for b in nodes:
-                radial = contract(TABLE.T, [radial_s[a, b] for a in nodes])
-                for a in nodes:
-                    value = image_raw[pair, a, b] + radial[a]
-                    image_raw[pair, a, b] = value
-                    product = product + residual[pair, a, b] * value
-            dots += [norm, product]
-        if turn < ITERS - 1:
-            across_layers()
-        sums, left, right = talk(turn + 1, dots)
-        for pair in pairs:
-            gamma, delta = (sums[2 * pair], sums[2 * pair + 1])
-            if turn == 0:
-                beta, inner = (None, delta)
-            else:
-                beta = gamma / gamma_old[pair]
-                inner = delta - beta * beta * inner_old[pair]
-            alpha = gamma / inner
-            gamma_old[pair], inner_old[pair] = (gamma, inner)
-            for a in nodes:
-                if turn < ITERS - 1:
                     start, end = across_columns(pair, a, left, right)
-                for b in nodes:
-                    now = residual[pair, a, b]
-                    if turn:
-                        now = now + beta * direction[pair, a, b]
-                    step = alpha * now
-                    total = step if turn == 0 else predicted[pair, a * NODES + b] + step
-                    if turn == ITERS - 1:
-                        for h in range(2):
-                            out[2 * pair + h, a * NODES + b] = total[h * LAYERS : (h + 1) * LAYERS]
-                    else:
-                        predicted[pair, a * NODES + b] = total
-                    if turn < ITERS - 1:
-                        direction[pair, a, b] = now
-                        image = start if b == 0 else end if b == NODES - 1 else image_raw[pair, a, b]
-                        if turn:
-                            image = image + beta * carried[pair, a, b]
-                        carried[pair, a, b] = image
-                        residual[pair, a, b] = residual[pair, a, b] - alpha * image
+                    for b in nodes:
+                        raw = image_raw[pair, a, b]
+                        residual[pair, a, b] = start if b == 0 else end if b == NODES - 1 else raw
+            if phase < ITERS:
+                dots = apply(pair)
+                if phase < ITERS - 1:
+                    across_layers(pair)
+                copies[pair] = post(phase + 1, pair, dots)
 
     for t in range(2):
         wait_all(posted[t], send_sem.at[0, t])
@@ -629,13 +634,13 @@
             field,
             slabs,
             slabs,
-            VMEM((ITERS + 1, ELEMS, 2, 8, LANES), jnp.float32),
-            VMEM((ITERS + 1, 2, 8, LANES), jnp.float32),
+            VMEM((ITERS + 1, OWN // 2, ELEMS, 8, LANES), jnp.float32),
+            VMEM((ITERS + 1, OWN // 2, 8, LANES), jnp.float32),
             DMA((10,)),
             DMA((2, 2)),
             DMA((2, 2)),
-            DMA((ITERS + 1, ELEMS)),
-            DMA((ITERS + 1, ELEMS)),
+            DMA((ITERS + 1, OWN // 2, ELEMS)),
+            DMA((ITERS + 1, OWN // 2, ELEMS)),
         ],
         compiler_params=pltpu.CompilerParams(
             collective_id=1, has_side_effects=True, vmem_limit_bytes=40 << 20

time: 85.7 us -> 85 us (level)
  no operation moved by 1% of the time
where the time goes in v3:
time: 85 us; the launch traced here: 84.9 us
  Pallas kernels  82.5 us (97%)
  local copies, waits for them, and re-layouts  1.77 us (2%)
    pallas_call x1, Pallas kernels, step_of(): pl.pallas_call(step_kernel, out_shape=(jax.ShapeDtypeStruct(velocity.shap...  82.5 us
    unnamed x2, local copies, waits for them, and re-layouts  1.77 us

profile of v3, /device:TPU:1, one launch (start us, length us, event | category | flops | bytes accessed | tf_op | source)
XLA Modules:
  0.0 84.9 jit_solution(16148658595479683498)
XLA Ops:
  0.6 82.5 %step.1 = (f32[2352,128]{1,0:T(8,128)S(1)}, f32[4,49,4,128]{3,2,1,0:T(4,128)S(1)}) custom-call(f32[2352,128]{1,0:T(8,128)} %bitcast.26, f32[49,4,128]{2,1,0:T(4,128)} %bitcast.27, f32[49,4,128]{2,1,0:T(4,128)} %bitcast.28, f32[49,4,128]{2,1,0:T(4,128)} %bitcast.29, f32[49,4,128]{2,1,0:T(4,128)} %bitcast.30, f32[49,4,128]{2,1,0:T(4,128)} %bitcast.31, ...), custom_call_target="tpu_custom_call" | custom-call | tf_op jit(solution)/shard_map/step/pallas_call | solution.py:603
  83.2 1.0 %copy.14 = f32[3,4,4,7,7,128]{5,2,4,3,1,0:T(4,128)} copy(f32[3,4,4,7,7,128]{5,2,4,3,1,0:T(4,128)S(1)} %bitcast.24) | data formatting | bytes 2408448
  84.2 0.7 copy.15
